TPU v7x, 128 devices: a whole 4x4x4 slice. The times are simulated.
128 devices in a mesh: seq: 32 (over x, y, core), tensor: 4 (over z).
Axes of the slice: x: 4, y: 4, z: 4, core: 2. Of those that a mesh axis runs over, the one named last changes fastest.
Arguments:
- tokens: bfloat16 [16384, 4096], P(('seq', 'tensor')), may hold values from -600 to 600
- gain: float32 [4096], replicated, may hold values from 0.5 to 1.5
- wq: bfloat16 [4096, 4096], P(None, 'tensor'), may hold values from -0.234375 to 0.234375
- wk: bfloat16 [4096, 1024], P(None, 'tensor'), may hold values from -0.09375 to 0.09375
- wv: bfloat16 [4096, 1024], P(None, 'tensor'), may hold values from -0.09375 to 0.09375
- wo: bfloat16 [4096, 4096], P('tensor'), may hold values from -0.25 to 0.25
- block_owner: int32 [128], replicated, may hold values from 0 to 32, as said below
Outputs:
- mixed: bfloat16 [16384, 4096], P(('seq', 'tensor'))
Inputs may be any that keep to these rules, and one draw needn't show every extreme that they name: `block_owner`: block b holds tokens b * 128 to (b + 1) * 128 - 1. The first blocks, between 32 and 64 of them, have owner 0; from there the owner starts at 1 and rises by 0 or 1 from block to block, each value above 0 being one tool call; there are exactly 32 tool calls.
All inputs are finite; a program needn't handle non-finite values.
Results may differ from a plain program's by a relative error of at most 0.017.
Values may be sent and summed in bfloat16 or wider, within the bound.
A program may use at most 192 MiB of HBM per device.

v0:
```python
import math

import jax
import jax.numpy as jnp
from jax import lax
from jax.sharding import PartitionSpec as P

HD = 128
BLK = 128


norm_eps = 1e-05
rope_base = 500000.0


def owner_of(position, owners):
    block_ids = jnp.arange(owners.shape[0], dtype=jnp.int32)
    matches = (position // BLK)[:, None] == block_ids[None, :]
    return jnp.sum(jnp.where(matches, owners[None, :], 0), axis=1)


def rope_position(position, owners):
    token_owner = owner_of(position, owners)
    context = BLK * jnp.sum((owners == 0).astype(jnp.int32))
    before = BLK * jnp.sum((owners[None, :] < token_owner[:, None]).astype(jnp.int32), axis=1)
    return jnp.where(token_owner == 0, position, context + position - before)


def rotate(vectors, position):
    half_size = vectors.shape[-1] // 2
    exponent = jnp.arange(half_size, dtype=jnp.float32) * (2.0 / vectors.shape[-1])
    frequency = jnp.exp(-exponent * math.log(rope_base))
    angles = position.astype(jnp.float32)[:, None] * frequency[None, :]
    cosine = jnp.cos(angles)[:, None, :]
    sine_part = jnp.sin(angles)[:, None, :]
    first_half = vectors[..., :half_size]
    second = vectors[..., half_size:]
    return jnp.concatenate(
        [first_half * cosine - second * sine_part, second * cosine + first_half * sine_part],
        axis=-1,
    )


def fresh_state(row_count, head_count, per_head):
    running_max = jnp.full((row_count, head_count, per_head), -1e30, jnp.float32)
    running_sum = jnp.zeros((row_count, head_count, per_head), jnp.float32)
    weighted = jnp.zeros((row_count, head_count, per_head, HD), jnp.float32)
    return (running_max, running_sum, weighted)


def absorb(softmax_state, queries, query_pos, query_owner, key_rows, value_rows, first_key, owners):
    key_count = key_rows.shape[0]
    key_pos = first_key + jnp.arange(key_count, dtype=jnp.int32)
    key_owner = owner_of(key_pos, owners)
    allowed = (key_pos[None, :] <= query_pos[:, None]) & (
        (key_owner[None, :] == 0) | (key_owner[None, :] == query_owner[:, None])
    )
    scale = 1.0 / math.sqrt(queries.shape[-1])

    def update(carried):
        running_max, running_sum, weighted = carried
        scores = (
            jnp.einsum("qhre,nhe->qhrn", queries, key_rows, preferred_element_type=jnp.float32)
            * scale
        )
        visible = allowed[:, None, None, :]
        scores = jnp.where(visible, scores, -1e30)
        new_max = jnp.maximum(running_max, jnp.max(scores, axis=-1))
        weights = jnp.where(visible, jnp.exp(scores - new_max[..., None]), 0.0)
        factor = jnp.exp(running_max - new_max)
        running_sum = running_sum * factor + jnp.sum(weights, axis=-1)
        weighted = weighted * factor[..., None] + jnp.einsum(
            "qhrn,nhe->qhre",
            weights.astype(jnp.bfloat16),
            value_rows,
            preferred_element_type=jnp.float32,
        )
        return (new_max, running_sum, weighted)

    return lax.cond(jnp.any(allowed), update, lambda carried: carried, softmax_state)


def finish(softmax_state):
    return (softmax_state[2] / softmax_state[1][..., None]).astype(jnp.bfloat16)


def per_device(tokens, gain, wq, wk, wv, wo, block_owner):
    tensor_count = lax.axis_size("tensor")
    seq_index = lax.axis_index("seq")
    local_rows = tokens.shape[0]
    tok_rows = local_rows * tensor_count
    q_heads = wq.shape[1] // HD
    kv_heads = wk.shape[1] // HD
    group_size = q_heads // kv_heads
    widened = tokens.astype(jnp.float32)
    normed = (
        widened * lax.rsqrt(jnp.mean(widened * widened, axis=-1, keepdims=True) + norm_eps) * gain
    ).astype(jnp.bfloat16)
    first_token = seq_index * tok_rows
    shard_part = lax.all_gather(normed, "tensor", axis=0, tiled=True)
    row_count = shard_part.shape[0]
    position = first_token + jnp.arange(row_count, dtype=jnp.int32)
    rotary = rope_position(position, block_owner)
    queries = rotate(
        jnp.dot(shard_part, wq, preferred_element_type=jnp.float32).reshape(row_count, q_heads, HD),
        rotary,
    ).astype(jnp.bfloat16)
    key_rows = rotate(
        jnp.dot(shard_part, wk, preferred_element_type=jnp.float32).reshape(
            row_count, kv_heads, HD
        ),
        rotary,
    ).astype(jnp.bfloat16)
    value_rows = jnp.dot(shard_part, wv, preferred_element_type=jnp.float32).astype(jnp.bfloat16)
    projected = jnp.concatenate(
        [
            queries.reshape(row_count, q_heads * HD),
            key_rows.reshape(row_count, kv_heads * HD),
            value_rows,
        ],
        axis=1,
    )
    queries = projected[:, : q_heads * HD].reshape(tok_rows, q_heads, HD)
    key_rows = projected[:, q_heads * HD : (q_heads + kv_heads) * HD].reshape(
        tok_rows, kv_heads, HD
    )
    value_rows = projected[:, (q_heads + kv_heads) * HD :].reshape(tok_rows, kv_heads, HD)
    grouped = queries.reshape(tok_rows, kv_heads, group_size, HD)
    query_pos = first_token + jnp.arange(tok_rows, dtype=jnp.int32)
    query_owner = owner_of(query_pos, block_owner)
    shard_part = lax.all_gather(
        jnp.stack((key_rows, value_rows), axis=1), "seq", axis=0, tiled=True
    )
    row_count = shard_part.shape[0]

    def sub_step(step_index, carried):
        key_block = lax.dynamic_slice_in_dim(shard_part, step_index * tok_rows, tok_rows, 0)
        return absorb(
            carried,
            grouped,
            query_pos,
            query_owner,
            key_block[:, 0],
            key_block[:, 1],
            step_index * tok_rows,
            block_owner,
        )

    softmax_state = lax.fori_loop(
        0, row_count // tok_rows, sub_step, fresh_state(tok_rows, kv_heads, group_size)
    )
    attended = finish(softmax_state).reshape(tok_rows, q_heads * HD)
    return lax.psum_scatter(
        jnp.dot(attended, wo, preferred_element_type=jnp.float32).astype(jnp.bfloat16),
        "tensor",
        scatter_dimension=0,
        tiled=True,
    )


def solution(mesh):
    in_specs = (
        P(("seq", "tensor"), None),
        P(),
        P(None, "tensor"),
        P(None, "tensor"),
        P(None, "tensor"),
        P("tensor", None),
        P(),
    )
    out_specs = P(("seq", "tensor"), None)
    return jax.shard_map(
        per_device, mesh=mesh, in_specs=in_specs, out_specs=out_specs, check_vma=False
    )
```

profile of v0, /device:TPU:4, one launch (start us, length us, event | category | flops | bytes accessed | tf_op | source)
XLA Modules:
  0.0 433.2 jit_solution(10586538848994207775)
XLA Ops:
  13.8 48.0 %all-gather.3.cloned.1.call-done = bf16[512,4096]{1,0:T(8,128)(2,1)} async-done(((bf16[128,4096]{1,0:T(8,128)(2,1)}), bf16[512,4096]{1,0:T(8,128)(2,1)}) %all-gather.3.cloned.1.call-update) | async-done | bytes 4194320 | tf_op jit(solution)/shard_map/all_gather | solution.py:100
  71.4 8.2 %convolution_bitcast_fusion = f32[64,8,8,128]{3,1,2,0:T(8,128)S(1)} fusion(bf16[512,4096]{1,0:T(8,128)(2,1)} %all-gather.3.cloned.1.call-done, bf16[4096,1024]{1,0:T(8,128)(2,1)} %param.13), kind=kOutput, calls=%fused_computation.42 | convolution fusion | flops 4294967296 | bytes 14680064 | tf_op jit(solution)/shard_map/dot_general | solution.py:105
  81.8 62.1 %all-gather.5.cloned.1.call-done = bf16[16384,2,2,128]{3,0,2,1:T(8,128)(2,1)} async-done(((bf16[512,2,2,128]{3,0,2,1:T(8,128)(2,1)}), bf16[16384,2,2,128]{3,0,2,1:T(8,128)(2,1)}) %all-gather.5.cloned.1.call-update) | async-done | bytes 16777232 | tf_op jit(solution)/shard_map/all_gather | solution.py:131
  144.0 213.6 %while.20 = (s32[]{:T(128)}, f32[512,2,4]{0,2,1:T(4,128)S(1)}, f32[512,2,4]{0,2,1:T(4,128)S(1)}, f32[512,2,4,128]{3,0,2,1:T(8,128)S(1)}, s32[128]{0:T(128)S(1)},...) while((s32[]{:T(128)}, f32[512,2,4]{0,2,1:T(4,128)S(1)}, ...), condition=%wide.region_11.12_spmd.clone, body=%wide.region_4.11_spmd.clone.sunk | while | flops 1103577600 | bytes 32266032 | solution.py:149
  145.9 9.0 %conditional.3 = ((f32[512,2,4]{0,2,1:T(4,128)S(1)}, f32[512,2,4]{0,2,1:T(4,128)S(1)}, f32[512,2,4,128]{3,0,2,1:T(8,128)S(1)})) conditional(s32[]{:T(128)} %convert_element_type.84, (f32[512,2,4]{0,2,1:T(4,128)S(1)}, f32[512,2,4]{0,2,1:T(4,128)S(1)}, f32[512,2,4,128]{3,0,2,1:T(8,128)S(1)}) %tuple.66, (pred[512,512]{0,1:T(8,128)(4,1)S(1)}, s32[]{:T(128)}, ...), branch_computations={%region_7.7_spmd, %region_8.10_spmd} | conditional | flops 1102061568 | bytes 31981658 | solution.py:80
  156.8 9.0 %conditional.3 = ((f32[512,2,4]{0,2,1:T(4,128)S(1)}, f32[512,2,4]{0,2,1:T(4,128)S(1)}, f32[512,2,4,128]{3,0,2,1:T(8,128)S(1)})) conditional(s32[]{:T(128)} %convert_element_type.84, (f32[512,2,4]{0,2,1:T(4,128)S(1)}, f32[512,2,4]{0,2,1:T(4,128)S(1)}, f32[512,2,4,128]{3,0,2,1:T(8,128)S(1)}) %tuple.66, (pred[512,512]{0,1:T(8,128)(4,1)S(1)}, s32[]{:T(128)}, ...), branch_computations={%region_7.7_spmd, %region_8.10_spmd} | conditional | flops 1102061568 | bytes 31981658 | solution.py:80
  167.7 9.0 %conditional.3 = ((f32[512,2,4]{0,2,1:T(4,128)S(1)}, f32[512,2,4]{0,2,1:T(4,128)S(1)}, f32[512,2,4,128]{3,0,2,1:T(8,128)S(1)})) conditional(s32[]{:T(128)} %convert_element_type.84, (f32[512,2,4]{0,2,1:T(4,128)S(1)}, f32[512,2,4]{0,2,1:T(4,128)S(1)}, f32[512,2,4,128]{3,0,2,1:T(8,128)S(1)}) %tuple.66, (pred[512,512]{0,1:T(8,128)(4,1)S(1)}, s32[]{:T(128)}, ...), branch_computations={%region_7.7_spmd, %region_8.10_spmd} | conditional | flops 1102061568 | bytes 31981658 | solution.py:80
  172.2 4.4 %bitcast_add_fusion = f32[512,2,4,128]{3,0,2,1:T(8,128)S(1)} fusion(f32[512,2,4,128]{3,0,2,1:T(8,128)S(1)} %get-tuple-element.291, f32[2,512,512,4]{2,1,3,0:T(8,128)S(1)} %get-tuple-element.356, f32[512,2,4]{0,2,1:T(4,128)S(1)} %max.3, pred[512,512]{0,1:T(8,128)(4,1)S(1)} %get-tuple-element.286, f32[512,2,4]{0,2,1:T(4,128)S(1)} %bitcast.66, ...), kind=kOutput, calls=%fused_computation.8 | convolution fusion | flops 548405248 | bytes 13139976 | tf_op jit(solution)/shard_map/while/body/eval_jaxpr/cond/branch_1_fun/qhrn,nhe->qhre/dot_general | solution.py:72
  178.6 9.0 %conditional.3 = ((f32[512,2,4]{0,2,1:T(4,128)S(1)}, f32[512,2,4]{0,2,1:T(4,128)S(1)}, f32[512,2,4,128]{3,0,2,1:T(8,128)S(1)})) conditional(s32[]{:T(128)} %convert_element_type.84, (f32[512,2,4]{0,2,1:T(4,128)S(1)}, f32[512,2,4]{0,2,1:T(4,128)S(1)}, f32[512,2,4,128]{3,0,2,1:T(8,128)S(1)}) %tuple.66, (pred[512,512]{0,1:T(8,128)(4,1)S(1)}, s32[]{:T(128)}, ...), branch_computations={%region_7.7_spmd, %region_8.10_spmd} | conditional | flops 1102061568 | bytes 31981658 | solution.py:80
  183.1 4.4 %bitcast_add_fusion = f32[512,2,4,128]{3,0,2,1:T(8,128)S(1)} fusion(f32[512,2,4,128]{3,0,2,1:T(8,128)S(1)} %get-tuple-element.291, f32[2,512,512,4]{2,1,3,0:T(8,128)S(1)} %get-tuple-element.356, f32[512,2,4]{0,2,1:T(4,128)S(1)} %max.3, pred[512,512]{0,1:T(8,128)(4,1)S(1)} %get-tuple-element.286, f32[512,2,4]{0,2,1:T(4,128)S(1)} %bitcast.66, ...), kind=kOutput, calls=%fused_computation.8 | convolution fusion | flops 548405248 | bytes 13139976 | tf_op jit(solution)/shard_map/while/body/eval_jaxpr/cond/branch_1_fun/qhrn,nhe->qhre/dot_general | solution.py:72
  189.5 9.0 %conditional.3 = ((f32[512,2,4]{0,2,1:T(4,128)S(1)}, f32[512,2,4]{0,2,1:T(4,128)S(1)}, f32[512,2,4,128]{3,0,2,1:T(8,128)S(1)})) conditional(s32[]{:T(128)} %convert_element_type.84, (f32[512,2,4]{0,2,1:T(4,128)S(1)}, f32[512,2,4]{0,2,1:T(4,128)S(1)}, f32[512,2,4,128]{3,0,2,1:T(8,128)S(1)}) %tuple.66, (pred[512,512]{0,1:T(8,128)(4,1)S(1)}, s32[]{:T(128)}, ...), branch_computations={%region_7.7_spmd, %region_8.10_spmd} | conditional | flops 1102061568 | bytes 31981658 | solution.py:80
  194.0 4.4 %bitcast_add_fusion = f32[512,2,4,128]{3,0,2,1:T(8,128)S(1)} fusion(f32[512,2,4,128]{3,0,2,1:T(8,128)S(1)} %get-tuple-element.291, f32[2,512,512,4]{2,1,3,0:T(8,128)S(1)} %get-tuple-element.356, f32[512,2,4]{0,2,1:T(4,128)S(1)} %max.3, pred[512,512]{0,1:T(8,128)(4,1)S(1)} %get-tuple-element.286, f32[512,2,4]{0,2,1:T(4,128)S(1)} %bitcast.66, ...), kind=kOutput, calls=%fused_computation.8 | convolution fusion | flops 548405248 | bytes 13139976 | tf_op jit(solution)/shard_map/while/body/eval_jaxpr/cond/branch_1_fun/qhrn,nhe->qhre/dot_general | solution.py:72
  200.4 9.0 %conditional.3 = ((f32[512,2,4]{0,2,1:T(4,128)S(1)}, f32[512,2,4]{0,2,1:T(4,128)S(1)}, f32[512,2,4,128]{3,0,2,1:T(8,128)S(1)})) conditional(s32[]{:T(128)} %convert_element_type.84, (f32[512,2,4]{0,2,1:T(4,128)S(1)}, f32[512,2,4]{0,2,1:T(4,128)S(1)}, f32[512,2,4,128]{3,0,2,1:T(8,128)S(1)}) %tuple.66, (pred[512,512]{0,1:T(8,128)(4,1)S(1)}, s32[]{:T(128)}, ...), branch_computations={%region_7.7_spmd, %region_8.10_spmd} | conditional | flops 1102061568 | bytes 31981658 | solution.py:80
  204.9 4.4 %bitcast_add_fusion = f32[512,2,4,128]{3,0,2,1:T(8,128)S(1)} fusion(f32[512,2,4,128]{3,0,2,1:T(8,128)S(1)} %get-tuple-element.291, f32[2,512,512,4]{2,1,3,0:T(8,128)S(1)} %get-tuple-element.356, f32[512,2,4]{0,2,1:T(4,128)S(1)} %max.3, pred[512,512]{0,1:T(8,128)(4,1)S(1)} %get-tuple-element.286, f32[512,2,4]{0,2,1:T(4,128)S(1)} %bitcast.66, ...), kind=kOutput, calls=%fused_computation.8 | convolution fusion | flops 548405248 | bytes 13139976 | tf_op jit(solution)/shard_map/while/body/eval_jaxpr/cond/branch_1_fun/qhrn,nhe->qhre/dot_general | solution.py:72
  211.3 9.0 %conditional.3 = ((f32[512,2,4]{0,2,1:T(4,128)S(1)}, f32[512,2,4]{0,2,1:T(4,128)S(1)}, f32[512,2,4,128]{3,0,2,1:T(8,128)S(1)})) conditional(s32[]{:T(128)} %convert_element_type.84, (f32[512,2,4]{0,2,1:T(4,128)S(1)}, f32[512,2,4]{0,2,1:T(4,128)S(1)}, f32[512,2,4,128]{3,0,2,1:T(8,128)S(1)}) %tuple.66, (pred[512,512]{0,1:T(8,128)(4,1)S(1)}, s32[]{:T(128)}, ...), branch_computations={%region_7.7_spmd, %region_8.10_spmd} | conditional | flops 1102061568 | bytes 31981658 | solution.py:80
  215.8 4.4 %bitcast_add_fusion = f32[512,2,4,128]{3,0,2,1:T(8,128)S(1)} fusion(f32[512,2,4,128]{3,0,2,1:T(8,128)S(1)} %get-tuple-element.291, f32[2,512,512,4]{2,1,3,0:T(8,128)S(1)} %get-tuple-element.356, f32[512,2,4]{0,2,1:T(4,128)S(1)} %max.3, pred[512,512]{0,1:T(8,128)(4,1)S(1)} %get-tuple-element.286, f32[512,2,4]{0,2,1:T(4,128)S(1)} %bitcast.66, ...), kind=kOutput, calls=%fused_computation.8 | convolution fusion | flops 548405248 | bytes 13139976 | tf_op jit(solution)/shard_map/while/body/eval_jaxpr/cond/branch_1_fun/qhrn,nhe->qhre/dot_general | solution.py:72
  222.1 9.0 %conditional.3 = ((f32[512,2,4]{0,2,1:T(4,128)S(1)}, f32[512,2,4]{0,2,1:T(4,128)S(1)}, f32[512,2,4,128]{3,0,2,1:T(8,128)S(1)})) conditional(s32[]{:T(128)} %convert_element_type.84, (f32[512,2,4]{0,2,1:T(4,128)S(1)}, f32[512,2,4]{0,2,1:T(4,128)S(1)}, f32[512,2,4,128]{3,0,2,1:T(8,128)S(1)}) %tuple.66, (pred[512,512]{0,1:T(8,128)(4,1)S(1)}, s32[]{:T(128)}, ...), branch_computations={%region_7.7_spmd, %region_8.10_spmd} | conditional | flops 1102061568 | bytes 31981658 | solution.py:80
  226.7 4.4 %bitcast_add_fusion = f32[512,2,4,128]{3,0,2,1:T(8,128)S(1)} fusion(f32[512,2,4,128]{3,0,2,1:T(8,128)S(1)} %get-tuple-element.291, f32[2,512,512,4]{2,1,3,0:T(8,128)S(1)} %get-tuple-element.356, f32[512,2,4]{0,2,1:T(4,128)S(1)} %max.3, pred[512,512]{0,1:T(8,128)(4,1)S(1)} %get-tuple-element.286, f32[512,2,4]{0,2,1:T(4,128)S(1)} %bitcast.66, ...), kind=kOutput, calls=%fused_computation.8 | convolution fusion | flops 548405248 | bytes 13139976 | tf_op jit(solution)/shard_map/while/body/eval_jaxpr/cond/branch_1_fun/qhrn,nhe->qhre/dot_general | solution.py:72
  233.0 9.0 %conditional.3 = ((f32[512,2,4]{0,2,1:T(4,128)S(1)}, f32[512,2,4]{0,2,1:T(4,128)S(1)}, f32[512,2,4,128]{3,0,2,1:T(8,128)S(1)})) conditional(s32[]{:T(128)} %convert_element_type.84, (f32[512,2,4]{0,2,1:T(4,128)S(1)}, f32[512,2,4]{0,2,1:T(4,128)S(1)}, f32[512,2,4,128]{3,0,2,1:T(8,128)S(1)}) %tuple.66, (pred[512,512]{0,1:T(8,128)(4,1)S(1)}, s32[]{:T(128)}, ...), branch_computations={%region_7.7_spmd, %region_8.10_spmd} | conditional | flops 1102061568 | bytes 31981658 | solution.py:80
  243.9 9.0 %conditional.3 = ((f32[512,2,4]{0,2,1:T(4,128)S(1)}, f32[512,2,4]{0,2,1:T(4,128)S(1)}, f32[512,2,4,128]{3,0,2,1:T(8,128)S(1)})) conditional(s32[]{:T(128)} %convert_element_type.84, (f32[512,2,4]{0,2,1:T(4,128)S(1)}, f32[512,2,4]{0,2,1:T(4,128)S(1)}, f32[512,2,4,128]{3,0,2,1:T(8,128)S(1)}) %tuple.66, (pred[512,512]{0,1:T(8,128)(4,1)S(1)}, s32[]{:T(128)}, ...), branch_computations={%region_7.7_spmd, %region_8.10_spmd} | conditional | flops 1102061568 | bytes 31981658 | solution.py:80
  254.8 9.0 %conditional.3 = ((f32[512,2,4]{0,2,1:T(4,128)S(1)}, f32[512,2,4]{0,2,1:T(4,128)S(1)}, f32[512,2,4,128]{3,0,2,1:T(8,128)S(1)})) conditional(s32[]{:T(128)} %convert_element_type.84, (f32[512,2,4]{0,2,1:T(4,128)S(1)}, f32[512,2,4]{0,2,1:T(4,128)S(1)}, f32[512,2,4,128]{3,0,2,1:T(8,128)S(1)}) %tuple.66, (pred[512,512]{0,1:T(8,128)(4,1)S(1)}, s32[]{:T(128)}, ...), branch_computations={%region_7.7_spmd, %region_8.10_spmd} | conditional | flops 1102061568 | bytes 31981658 | solution.py:80
  265.7 9.0 %conditional.3 = ((f32[512,2,4]{0,2,1:T(4,128)S(1)}, f32[512,2,4]{0,2,1:T(4,128)S(1)}, f32[512,2,4,128]{3,0,2,1:T(8,128)S(1)})) conditional(s32[]{:T(128)} %convert_element_type.84, (f32[512,2,4]{0,2,1:T(4,128)S(1)}, f32[512,2,4]{0,2,1:T(4,128)S(1)}, f32[512,2,4,128]{3,0,2,1:T(8,128)S(1)}) %tuple.66, (pred[512,512]{0,1:T(8,128)(4,1)S(1)}, s32[]{:T(128)}, ...), branch_computations={%region_7.7_spmd, %region_8.10_spmd} | conditional | flops 1102061568 | bytes 31981658 | solution.py:80
  270.3 4.4 %bitcast_add_fusion = f32[512,2,4,128]{3,0,2,1:T(8,128)S(1)} fusion(f32[512,2,4,128]{3,0,2,1:T(8,128)S(1)} %get-tuple-element.291, f32[2,512,512,4]{2,1,3,0:T(8,128)S(1)} %get-tuple-element.356, f32[512,2,4]{0,2,1:T(4,128)S(1)} %max.3, pred[512,512]{0,1:T(8,128)(4,1)S(1)} %get-tuple-element.286, f32[512,2,4]{0,2,1:T(4,128)S(1)} %bitcast.66, ...), kind=kOutput, calls=%fused_computation.8 | convolution fusion | flops 548405248 | bytes 13139976 | tf_op jit(solution)/shard_map/while/body/eval_jaxpr/cond/branch_1_fun/qhrn,nhe->qhre/dot_general | solution.py:72
  276.6 9.0 %conditional.3 = ((f32[512,2,4]{0,2,1:T(4,128)S(1)}, f32[512,2,4]{0,2,1:T(4,128)S(1)}, f32[512,2,4,128]{3,0,2,1:T(8,128)S(1)})) conditional(s32[]{:T(128)} %convert_element_type.84, (f32[512,2,4]{0,2,1:T(4,128)S(1)}, f32[512,2,4]{0,2,1:T(4,128)S(1)}, f32[512,2,4,128]{3,0,2,1:T(8,128)S(1)}) %tuple.66, (pred[512,512]{0,1:T(8,128)(4,1)S(1)}, s32[]{:T(128)}, ...), branch_computations={%region_7.7_spmd, %region_8.10_spmd} | conditional | flops 1102061568 | bytes 31981658 | solution.py:80
  281.2 4.4 %bitcast_add_fusion = f32[512,2,4,128]{3,0,2,1:T(8,128)S(1)} fusion(f32[512,2,4,128]{3,0,2,1:T(8,128)S(1)} %get-tuple-element.291, f32[2,512,512,4]{2,1,3,0:T(8,128)S(1)} %get-tuple-element.356, f32[512,2,4]{0,2,1:T(4,128)S(1)} %max.3, pred[512,512]{0,1:T(8,128)(4,1)S(1)} %get-tuple-element.286, f32[512,2,4]{0,2,1:T(4,128)S(1)} %bitcast.66, ...), kind=kOutput, calls=%fused_computation.8 | convolution fusion | flops 548405248 | bytes 13139976 | tf_op jit(solution)/shard_map/while/body/eval_jaxpr/cond/branch_1_fun/qhrn,nhe->qhre/dot_general | solution.py:72
  287.5 9.0 %conditional.3 = ((f32[512,2,4]{0,2,1:T(4,128)S(1)}, f32[512,2,4]{0,2,1:T(4,128)S(1)}, f32[512,2,4,128]{3,0,2,1:T(8,128)S(1)})) conditional(s32[]{:T(128)} %convert_element_type.84, (f32[512,2,4]{0,2,1:T(4,128)S(1)}, f32[512,2,4]{0,2,1:T(4,128)S(1)}, f32[512,2,4,128]{3,0,2,1:T(8,128)S(1)}) %tuple.66, (pred[512,512]{0,1:T(8,128)(4,1)S(1)}, s32[]{:T(128)}, ...), branch_computations={%region_7.7_spmd, %region_8.10_spmd} | conditional | flops 1102061568 | bytes 31981658 | solution.py:80
  292.1 4.4 %bitcast_add_fusion = f32[512,2,4,128]{3,0,2,1:T(8,128)S(1)} fusion(f32[512,2,4,128]{3,0,2,1:T(8,128)S(1)} %get-tuple-element.291, f32[2,512,512,4]{2,1,3,0:T(8,128)S(1)} %get-tuple-element.356, f32[512,2,4]{0,2,1:T(4,128)S(1)} %max.3, pred[512,512]{0,1:T(8,128)(4,1)S(1)} %get-tuple-element.286, f32[512,2,4]{0,2,1:T(4,128)S(1)} %bitcast.66, ...), kind=kOutput, calls=%fused_computation.8 | convolution fusion | flops 548405248 | bytes 13139976 | tf_op jit(solution)/shard_map/while/body/eval_jaxpr/cond/branch_1_fun/qhrn,nhe->qhre/dot_general | solution.py:72
  298.4 9.0 %conditional.3 = ((f32[512,2,4]{0,2,1:T(4,128)S(1)}, f32[512,2,4]{0,2,1:T(4,128)S(1)}, f32[512,2,4,128]{3,0,2,1:T(8,128)S(1)})) conditional(s32[]{:T(128)} %convert_element_type.84, (f32[512,2,4]{0,2,1:T(4,128)S(1)}, f32[512,2,4]{0,2,1:T(4,128)S(1)}, f32[512,2,4,128]{3,0,2,1:T(8,128)S(1)}) %tuple.66, (pred[512,512]{0,1:T(8,128)(4,1)S(1)}, s32[]{:T(128)}, ...), branch_computations={%region_7.7_spmd, %region_8.10_spmd} | conditional | flops 1102061568 | bytes 31981658 | solution.py:80
  309.3 9.0 %conditional.3 = ((f32[512,2,4]{0,2,1:T(4,128)S(1)}, f32[512,2,4]{0,2,1:T(4,128)S(1)}, f32[512,2,4,128]{3,0,2,1:T(8,128)S(1)})) conditional(s32[]{:T(128)} %convert_element_type.84, (f32[512,2,4]{0,2,1:T(4,128)S(1)}, f32[512,2,4]{0,2,1:T(4,128)S(1)}, f32[512,2,4,128]{3,0,2,1:T(8,128)S(1)}) %tuple.66, (pred[512,512]{0,1:T(8,128)(4,1)S(1)}, s32[]{:T(128)}, ...), branch_computations={%region_7.7_spmd, %region_8.10_spmd} | conditional | flops 1102061568 | bytes 31981658 | solution.py:80
  320.2 9.0 %conditional.3 = ((f32[512,2,4]{0,2,1:T(4,128)S(1)}, f32[512,2,4]{0,2,1:T(4,128)S(1)}, f32[512,2,4,128]{3,0,2,1:T(8,128)S(1)})) conditional(s32[]{:T(128)} %convert_element_type.84, (f32[512,2,4]{0,2,1:T(4,128)S(1)}, f32[512,2,4]{0,2,1:T(4,128)S(1)}, f32[512,2,4,128]{3,0,2,1:T(8,128)S(1)}) %tuple.66, (pred[512,512]{0,1:T(8,128)(4,1)S(1)}, s32[]{:T(128)}, ...), branch_computations={%region_7.7_spmd, %region_8.10_spmd} | conditional | flops 1102061568 | bytes 31981658 | solution.py:80
  361.4 9.6 %convolution_convert_fusion = bf16[512,4096]{1,0:T(8,128)(2,1)} fusion(bf16[512,1024]{0,1:T(8,128)(2,1)S(1)} %bitcast.62, bf16[1024,4096]{1,0:T(8,128)(2,1)} %param.16), kind=kOutput, calls=%fused_computation.33 | convolution fusion | flops 4297064448 | bytes 13631488 | tf_op jit(solution)/shard_map/dot_general | solution.py:154
  371.0 55.6 %reduce-scatter.2.cloned.1.call-done = bf16[128,4096]{1,0:T(8,128)(2,1)} async-done(((bf16[512,4096]{1,0:T(8,128)(2,1)}), bf16[128,4096]{1,0:T(8,128)(2,1)}) %reduce-scatter.2.cloned.1.call-update) | async-done | bytes 1048592 | tf_op jit(solution)/shard_map/reduce_scatter | solution.py:153
  (308 shorter events, 175.3 us)
Async XLA Ops:
  6.5 55.2 %copy-start = (bf16[4096,256]{1,0:T(8,128)(2,1)S(1)}, bf16[4096,256]{1,0:T(8,128)(2,1)}, u32[]{:S(2)}) copy-start(bf16[4096,256]{1,0:T(8,128)(2,1)} %param.15) | copy-start | bytes 6291460
  6.5 4.3 copy-start.2
  6.5 55.2 %all-gather.3.cloned.1.call-start = ((), (), s32[]{:S(2)}) async-start(), calls=%async_computation.1 | async-start | bytes 5242880 | tf_op jit(solution)/shard_map/all_gather | solution.py:100
  10.8 133.1 %all-gather.5.cloned.1.call-start = ((), (), s32[]{:S(2)}) async-start(), calls=%async_computation.2 | async-start | bytes 17301504 | tf_op jit(solution)/shard_map/all_gather | solution.py:131
  71.2 355.5 %reduce-scatter.2.cloned.1.call-start = ((), (), s32[]{:S(2)}) async-start(), calls=%async_computation.3 | async-start | bytes 5242880 | tf_op jit(solution)/shard_map/reduce_scatter | solution.py:153
  361.4 65.3 %copy-start.1 = (bf16[4096,256]{1,0:T(8,128)(2,1)S(1)}, bf16[4096,256]{1,0:T(8,128)(2,1)}, u32[]{:S(2)}) copy-start(bf16[4096,256]{1,0:T(8,128)(2,1)} %param.15) | copy-start | bytes 6291460
Sparse Core Ops, SparseCore 0:
  10.9 50.8 all-gather.2
  71.3 72.5 all-gather.4
  371.1 55.4 reduce-scatter.1
where the time goes:
time: 427 us; the launch traced here: 433 us
  waiting for transfers between devices  166 us (39%)
  matrix products  143 us (33%)
  other arithmetic  86.4 us (20%)
  loops' own time  20.8 us (5%)
  between operations  14 us (3%)
    dot_general x17, matrix products, update(): jnp.einsum('qhrn,nhe->qhre', weights.astype(jnp.bfloat16), value_rows, pr...  75.3 us
    all_gather x1, waiting for transfers between devices, per_device(): lax.all_gather(jnp.stack((key_rows, value_rows), axis=1), 'seq', axis=0,...  62.1 us
    reduce_scatter x1, waiting for transfers between devices, per_device(): lax.psum_scatter(jnp.dot(attended, wo, preferred_element_type=jnp.float32...  55.6 us
    all_gather x1, waiting for transfers between devices, per_device(): shard_part = lax.all_gather(normed, 'tensor', axis=0, tiled=True)  48 us
    dot_general x17, matrix products, update(): jnp.einsum('qhre,nhe->qhrn', queries, key_rows, preferred_element_type=jn...  41.9 us
    reduce_sum x17, other arithmetic, update(): running_sum = running_sum * factor + jnp.sum(weights, axis=-1)  34.7 us
    reduce_or x32, other arithmetic, absorb(): jnp.any(allowed)  32.3 us
    another operation x1, loops' own time, per_device(): lax.fori_loop(0, row_count // tok_rows, sub_step, fresh_state(tok_rows, k...  19.5 us
  transfers between devices with their start and end apart: 3, of which 3 were waited for; matrix products, arithmetic and copies ran while one was open for 3% of the time, Pallas kernels for 0%

commit v1 on v0

v1 whole, which is shorter than its diff:
```python
import functools
import math

import jax
import jax.numpy as jnp
from jax import lax
from jax.experimental import pallas as pl
from jax.experimental.layout import Layout, with_layout_constraint
from jax.experimental.pallas import tpu as pltpu
from jax.sharding import PartitionSpec as P

HD = 128
BLK = 128
LOWEST = -1e30


norm_eps = 1e-05
rope_base = 500000.0


def owner_of(position, owners):
    block_ids = jnp.arange(owners.shape[0], dtype=jnp.int32)
    matches = (position // BLK)[:, None] == block_ids[None, :]
    return jnp.sum(jnp.where(matches, owners[None, :], 0), axis=1)


def rope_position(position, owners):
    token_owner = owner_of(position, owners)
    context = BLK * jnp.sum((owners == 0).astype(jnp.int32))
    before = BLK * jnp.sum((owners[None, :] < token_owner[:, None]).astype(jnp.int32), axis=1)
    return jnp.where(token_owner == 0, position, context + position - before)


def rotate(vectors, position):
    half_size = vectors.shape[-1] // 2
    exponent = jnp.arange(half_size, dtype=jnp.float32) * (2.0 / vectors.shape[-1])
    frequency = jnp.exp(-exponent * math.log(rope_base))
    angles = position.astype(jnp.float32)[:, None] * frequency[None, :]
    cosine = jnp.cos(angles)[:, None, :]
    sine_part = jnp.sin(angles)[:, None, :]
    first_half = vectors[..., :half_size]
    second = vectors[..., half_size:]
    return jnp.concatenate(
        [first_half * cosine - second * sine_part, second * cosine + first_half * sine_part],
        axis=-1,
    )


def attend_kernel(plan_ref, q_hbm, kv_hbm, wo_hbm, o_ref, qbuf, kvbuf, wobuf, acc, total_s, max_s, kv_sems, q_sem, wo_sem, *, full_blocks, tail_blocks, rows_per_step):
    context, first_own, count, last, row = [plan_ref[i] for i in range(5)]
    heads = qbuf.shape[1] // HD
    groups = kvbuf.shape[3] // (2 * HD)
    per_group = heads // groups
    full_steps = (count - 1) // full_blocks
    rest = count - full_steps * full_blocks
    steps = full_steps + (rest + tail_blocks - 1) // tail_blocks
    wo_copy = pltpu.make_async_copy(wo_hbm, wobuf, wo_sem)
    q_copy = pltpu.make_async_copy(q_hbm.at[pl.ds(pl.multiple_of(row, BLK), BLK)], qbuf, q_sem)

    def start_of(step):
        return jnp.where(step < full_steps, step * full_blocks, full_steps * full_blocks + (step - full_steps) * tail_blocks)

    def fetch(step, slot):
        base = start_of(step)

        def one(j):
            at = base + j
            block = jnp.where(at < context, at, jnp.minimum(first_own + at - context, last))
            pltpu.make_async_copy(kv_hbm.at[block], kvbuf.at[slot, j], kv_sems.at[slot]).start()

        for j in range(tail_blocks):
            one(j)

        if full_blocks > tail_blocks:
            @pl.when(step < full_steps)
            def _():
                for j in range(tail_blocks, full_blocks):
                    one(j)

    q_copy.start()
    fetch(0, 0)
    wo_copy.start()
    acc[...] = jnp.zeros_like(acc)
    total_s[...] = jnp.zeros_like(total_s)
    max_s[...] = jnp.full_like(max_s, LOWEST)
    q_copy.wait()

    def absorb(step, blocks, masked):
        slot = lax.rem(step, 2)

        @pl.when(step + 1 < steps)
        def _():
            fetch(step + 1, 1 - slot)

        pltpu.make_async_copy(kv_hbm.at[pl.ds(0, blocks)], kvbuf.at[slot, pl.ds(0, blocks)], kv_sems.at[slot]).wait()
        keys = blocks * BLK
        if masked:
            column = lax.broadcasted_iota(jnp.int32, (BLK, keys), 1) + (start_of(step) - (count - 1)) * BLK
            visible = column <= lax.broadcasted_iota(jnp.int32, (BLK, keys), 0)
            visible = jnp.concatenate([visible] * rows_per_step, axis=0)
        for g in range(groups):
            k = kvbuf[slot, :blocks, :, g * HD:(g + 1) * HD].reshape(keys, HD)
            v = kvbuf[slot, :blocks, :, (groups + g) * HD:(groups + g + 1) * HD].reshape(keys, HD)
            v_one = jnp.concatenate([v, jnp.ones_like(v)], axis=1)
            for first in range(g * per_group, (g + 1) * per_group, rows_per_step):
                q = jnp.concatenate([qbuf[:, h * HD:(h + 1) * HD] for h in range(first, first + rows_per_step)], axis=0)
                s = lax.dot_general(q, k, (((1,), (1,)), ((), ())), preferred_element_type=jnp.float32)
                if masked:
                    s = jnp.where(visible, s, LOWEST)
                rows = pl.ds(first * BLK, rows_per_step * BLK)
                top = s[:, :BLK]
                for j in range(1, blocks):
                    top = jnp.maximum(top, s[:, j * BLK:(j + 1) * BLK])
                old = max_s[rows]
                new = jnp.maximum(old, jnp.max(top, axis=1, keepdims=True))
                factor = jnp.exp2(old - new)
                p = jnp.concatenate([jnp.exp2(s[:, j * BLK:(j + 1) * BLK] - new).astype(jnp.bfloat16) for j in range(blocks)], axis=1)
                r = jnp.dot(p, v_one, preferred_element_type=jnp.float32)
                acc[rows] = acc[rows] * factor + r[:, :HD]
                total_s[rows] = total_s[rows] * factor + r[:, HD:]
                max_s[rows] = new

    def full(step, carry):
        absorb(step, full_blocks, False)
        return carry

    def tail(step, carry):
        absorb(step, tail_blocks, True)
        return carry

    lax.fori_loop(0, full_steps, full, 0)
    lax.fori_loop(full_steps, steps, tail, 0)
    attended = jnp.concatenate(
        [(acc[pl.ds(h * BLK, BLK)] / total_s[pl.ds(h * BLK, BLK)]).astype(jnp.bfloat16) for h in range(heads)], axis=1)
    wo_copy.wait()
    o_ref[...] = jnp.dot(attended, wobuf[...], preferred_element_type=jnp.float32).astype(jnp.bfloat16)


def attend(plan, q, kv, wo, full_blocks=16, tail_blocks=4, rows_per_step=2):
    width = wo.shape[1]
    heads = q.shape[1] // HD
    any_space = pl.BlockSpec(memory_space=pl.ANY)
    state = pltpu.VMEM((heads * BLK, HD), jnp.float32)
    return pl.pallas_call(
        functools.partial(attend_kernel, full_blocks=full_blocks, tail_blocks=tail_blocks, rows_per_step=rows_per_step),
        out_shape=jax.ShapeDtypeStruct((BLK, width), jnp.bfloat16),
        in_specs=[pl.BlockSpec(memory_space=pltpu.SMEM), any_space, any_space, any_space],
        out_specs=pl.BlockSpec(memory_space=pltpu.VMEM),
        scratch_shapes=[
            pltpu.VMEM((BLK, heads * HD), jnp.bfloat16),
            pltpu.VMEM((2, full_blocks, BLK, kv.shape[2]), jnp.bfloat16),
            pltpu.VMEM(wo.shape, jnp.bfloat16),
            state, state, state,
            pltpu.SemaphoreType.DMA((2,)),
            pltpu.SemaphoreType.DMA,
            pltpu.SemaphoreType.DMA,
        ],
        compiler_params=pltpu.CompilerParams(vmem_limit_bytes=56 * 1024 * 1024),
        cost_estimate=pl.CostEstimate(flops=8 * heads * BLK * 6400 * HD, bytes_accessed=16 << 20, transcendentals=heads * BLK * 6400),
    )(plan, q, kv, wo)


def plan_of(block, row, owners):
    owner = jnp.sum(jnp.where(jnp.arange(owners.shape[0]) == block, owners, 0))
    shared = jnp.sum((owners == 0).astype(jnp.int32))
    first_own = jnp.sum((owners < owner).astype(jnp.int32))
    context = jnp.where(owner == 0, block + 1, shared)
    count = jnp.where(owner == 0, block + 1, shared + block - first_own + 1)
    return jnp.stack([context, first_own, count, block, row]).astype(jnp.int32)


def per_device(tokens, gain, wq, wk, wv, wo, block_owner):
    parts = lax.axis_size("tensor")
    seq_index = lax.axis_index("seq")
    part = lax.axis_index("tensor")
    local_rows = tokens.shape[0]
    tok_rows = local_rows * parts
    q_heads = wq.shape[1] // HD
    kv_heads = wk.shape[1] // HD
    widened = tokens.astype(jnp.float32)
    normed = (
        widened * lax.rsqrt(jnp.mean(widened * widened, axis=-1, keepdims=True) + norm_eps) * gain
    ).astype(jnp.bfloat16)
    rows = lax.all_gather(normed, "tensor", axis=0, tiled=True)
    position = seq_index * tok_rows + jnp.arange(tok_rows, dtype=jnp.int32)
    rotary = rope_position(position, block_owner)
    keys = rotate(
        jnp.dot(rows, wk, preferred_element_type=jnp.float32).reshape(tok_rows, kv_heads, HD), rotary
    ).astype(jnp.bfloat16)
    values = jnp.dot(rows, wv, preferred_element_type=jnp.float32).astype(jnp.bfloat16)
    own = jnp.concatenate([keys.reshape(tok_rows, kv_heads * HD), values], axis=1)
    own = with_layout_constraint(own, Layout(major_to_minor=(0, 1)))
    gathered = lax.all_gather(own, "seq", axis=0, tiled=True)
    queries = rotate(
        jnp.dot(rows, wq, preferred_element_type=jnp.float32).reshape(tok_rows, q_heads, HD), rotary
    )
    queries = (queries * (math.log2(math.e) / math.sqrt(HD))).astype(jnp.bfloat16)
    queries = queries.reshape(tok_rows, q_heads * HD)
    kv = gathered.reshape(-1, BLK, own.shape[1])
    total = None
    pieces = []
    for shift in (2, 1, 3, 0):
        group = lax.rem(part + shift, parts)
        plan = plan_of(seq_index * parts + group, group * BLK, block_owner)
        piece = attend(plan, queries, kv, wo)
        if shift:
            piece = lax.ppermute(piece, "tensor", [(i, (i + shift) % parts) for i in range(parts)])
        pieces.append(piece)
    total = sum(piece.astype(jnp.float32) for piece in pieces[::-1])
    return total.astype(jnp.bfloat16)


def solution(mesh):
    in_specs = (
        P(("seq", "tensor"), None),
        P(),
        P(None, "tensor"),
        P(None, "tensor"),
        P(None, "tensor"),
        P("tensor", None),
        P(),
    )
    out_specs = P(("seq", "tensor"), None)
    return jax.shard_map(
        per_device, mesh=mesh, in_specs=in_specs, out_specs=out_specs, check_vma=False
    )
```

time: 427 us -> 230 us (0.54); the launches traced: 433 us -> 229 us
  matrix products: 143 us -> 15.1 us
  other arithmetic: 86.4 us -> 17 us
  waiting for transfers between devices: 166 us -> 97.8 us
  Pallas kernels: 0 us -> 60.5 us
  loops' own time: 20.8 us -> 0 us
  between operations: 14 us -> 24.7 us
  starting transfers between devices: 0.27 us -> 6.66 us
    dot_general x38 -> x3, matrix products: 143 us -> 15.1 us  [the longest x1 8.15 us: per_device(): jnp.dot(rows, wq, preferred_element_type=jnp.float32)]
    pallas_call x0 -> x4, Pallas kernels: none -> 60.5 us  [attend(): pl.pallas_call(functools.partial(attend_kernel, full_blocks=full_blocks,...]
    reduce_scatter x1 -> x0, waiting for transfers between devices: 55.6 us -> none  [per_device(): lax.psum_scatter(jnp.dot(attended, wo, preferred_element_type=jnp.float32...]
    reduce_or x32 -> x0, other arithmetic: 32.3 us -> none  [absorb(): jnp.any(allowed)]
    reduce_sum x18 -> x2, other arithmetic: 35.4 us -> 4.01 us  [the longest x1 3.26 us: plan_of(): first_own = jnp.sum((owners < owner).astype(jnp.int32))]
    another operation x33 -> x0, loops' own time: 20.8 us -> none  [the longest x1 19.5 us: per_device(): lax.fori_loop(0, row_count // tok_rows, sub_step, fresh_state(tok_rows, k...]
    all_gather x2, waiting for transfers between devices: 110 us -> 94.3 us  [the longest x1 49.6 us: per_device(): gathered = lax.all_gather(own, 'seq', axis=0, tiled=True)]
    reduce_sum x33 -> x1, other arithmetic: 7.66 us -> 0.23 us  [owner_of(): return jnp.sum(jnp.where(matches, owners[None, :], 0), axis=1)]
  transfers between devices with their start and end apart: 3 -> 5, of which waited for: 3 -> 3; matrix products, arithmetic and copies ran while one was open for 3% -> 10% of each run, Pallas kernels for 0% -> 20%
where the time goes in v1:
time: 230 us; the launch traced here: 229 us
  waiting for transfers between devices  97.8 us (43%)
  Pallas kernels  60.5 us (26%)
  between operations  24.7 us (11%)
  other arithmetic  17 us (7%)
  matrix products  15.1 us (7%)
  local copies, waits for them, and re-layouts  7.5 us (3%)
  starting transfers between devices  6.66 us (3%)
    pallas_call x4, Pallas kernels, attend(): pl.pallas_call(functools.partial(attend_kernel, full_blocks=full_blocks,...  60.5 us
    all_gather x1, waiting for transfers between devices, per_device(): gathered = lax.all_gather(own, 'seq', axis=0, tiled=True)  49.6 us
    all_gather x1, waiting for transfers between devices, per_device(): rows = lax.all_gather(normed, 'tensor', axis=0, tiled=True)  44.7 us
    dot_general x1, matrix products, per_device(): jnp.dot(rows, wq, preferred_element_type=jnp.float32)  8.15 us
    ppermute x3, starting transfers between devices, per_device(): lax.ppermute(piece, 'tensor', [(i, (i + shift) % parts) for i in range(pa...  6.62 us
    another operation x4, local copies, waits for them, and re-layouts, plan_of(): return jnp.stack([context, first_own, count, block, row]).astype(jnp.int32)  4.96 us
  transfers between devices with their start and end apart: 5, of which 3 were waited for; matrix products, arithmetic and copies ran while one was open for 10% of the time, Pallas kernels for 20%

profile of v1, /device:TPU:4, one launch (start us, length us, event | category | flops | bytes accessed | tf_op | source)
XLA Modules:
  0.0 229.2 jit_solution(8079307898358009349)
XLA Ops:
  6.5 1.7 fusion
  8.2 2.5 %fusion.2 = bf16[128,4096]{1,0:T(8,128)(2,1)} fusion(bf16[128,4096]{1,0:T(8,128)(2,1)} %param.7, f32[4096]{0:T(1024)} %param.8, f32[128]{0:T(128)S(1)} %add_rsqrt_fusion), kind=kLoop, calls=%fused_computation.4 | loop fusion | flops 2097152 | bytes 2114048 | tf_op jit(solution)/shard_map/convert_element_type | solution.py:183
  10.9 0.8 fusion.7
  11.6 3.3 %fusion.9 = (s32[]{:T(128)}, s32[]{:T(128)}, s32[]{:T(128)}, s32[]{:T(128)}, s32[]{:T(128)}) fusion(s32[128]{0:T(128)S(1)} %copy-done.2, s32[]{:T(128)} %get-tuple-element.10, s32[]{:T(128)} %get-tuple-element.11, s32[]{:T(128)} %get-tuple-element.12, s32[]{:T(128)} %get-tuple-element.13), kind=kLoop, calls=%fused_computation.44 | loop fusion | flops 1915 | bytes 548 | tf_op jit(solution)/shard_map/reduce_sum | solution.py:166
  15.8 0.2 convert_reduce_fusion
  16.1 1.0 multiply_cosine_fusion
  17.1 44.7 %all-gather.3.cloned.1.call-done = bf16[512,4096]{1,0:T(8,128)(2,1)} async-done(((bf16[128,4096]{1,0:T(8,128)(2,1)}), bf16[512,4096]{1,0:T(8,128)(2,1)}) %all-gather.3.cloned.1.call-update) | async-done | bytes 4194320 | tf_op jit(solution)/shard_map/all_gather | solution.py:184
  61.8 3.5 %fusion.17 = f32[512,256]{0,1:T(8,128)S(1)} fusion(bf16[512,4096]{1,0:T(8,128)(2,1)} %all-gather.3.cloned.1.call-done, bf16[4096,256]{1,0:T(8,128)(2,1)S(1)} %copy-done), kind=kOutput, calls=%fused_computation.54 | convolution fusion | flops 1073741824 | bytes 6815744 | tf_op jit(solution)/shard_map/dot_general | solution.py:188
  65.8 0.5 subtract_convert_fusion
  66.3 0.7 pad_maximum_fusion.1
  67.1 0.3 copy-done.3
  67.4 3.5 %convolution_convert_fusion = bf16[512,256]{1,0:T(8,128)(2,1)S(1)} fusion(bf16[512,4096]{1,0:T(8,128)(2,1)} %all-gather.3.cloned.1.call-done, bf16[4096,256]{1,0:T(8,128)(2,1)S(1)} %copy-done.3), kind=kOutput, calls=%fused_computation.11 | convolution fusion | flops 1073872896 | bytes 6553600 | tf_op jit(solution)/shard_map/dot_general | solution.py:190
  70.8 0.8 pad_maximum_fusion
  79.5 1.3 stack.95.plan_ref
  80.8 1.3 stack.89.plan_ref
  82.1 1.1 stack.83.plan_ref
  83.2 8.2 %convolution_bitcast_fusion = f32[64,8,8,128]{3,1,2,0:T(8,128)S(1)} fusion(bf16[512,4096]{1,0:T(8,128)(2,1)} %all-gather.3.cloned.1.call-done, bf16[4096,1024]{1,0:T(8,128)(2,1)} %param.9), kind=kOutput, calls=%fused_computation.10 | convolution fusion | flops 4294967296 | bytes 14680064 | tf_op jit(solution)/shard_map/dot_general | solution.py:195
  91.4 0.5 copy.17
  91.9 1.1 multiply_subtract_fusion
  93.0 0.6 fusion.3
  93.6 1.2 copy.22
  94.9 49.6 %all-gather.5.cloned.1.call-done = bf16[16384,512]{1,0:T(8,128)(2,1)} async-done(((bf16[512,512]{1,0:T(8,128)(2,1)}), bf16[16384,512]{1,0:T(8,128)(2,1)}) %all-gather.5.cloned.1.call-update) | async-done | bytes 16777232 | tf_op jit(solution)/shard_map/all_gather | solution.py:193
  144.4 15.1 %shard_map.76 = bf16[128,4096]{1,0:T(8,128)(2,1)} custom-call(s32[5]{0:T(128)} %stack.95.plan_ref, bf16[512,1024]{1,0:T(8,128)(2,1)} %bitcast.43, bf16[128,128,512]{2,1,0:T(8,128)(2,1)} %bitcast.39, bf16[1024,4096]{1,0:T(8,128)(2,1)} %wo_hbm.7), custom_call_target="tpu_custom_call" | custom-call | flops 6710886400 | bytes 16777216 | tf_op jit(solution)/shard_map/pallas_call | solution.py:144
  159.5 3.2 %collective-permute-start.2 = (bf16[128,4096]{1,0:T(8,128)(2,1)}, bf16[128,4096]{1,0:T(8,128)(2,1)S(1)}, u32[]{:S(2)}, u32[]{:S(2)}) collective-permute-start(bf16[128,4096]{1,0:T(8,128)(2,1)} %shard_map.76), channel_id=1, source_target_pairs={{0,2},{1,3},{2,0},{3,1},{4,6},{5,7},{6,4},{7,5},{8,10},{9,11},{10,... | collective-permute-start | bytes 3145736 | tf_op jit(solution)/shard_map/ppermute | solution.py:207
  162.7 15.1 %shard_map.75 = bf16[128,4096]{1,0:T(8,128)(2,1)} custom-call(s32[5]{0:T(128)} %stack.89.plan_ref, bf16[512,1024]{1,0:T(8,128)(2,1)} %bitcast.44, bf16[128,128,512]{2,1,0:T(8,128)(2,1)} %bitcast.40, bf16[1024,4096]{1,0:T(8,128)(2,1)} %wo_hbm.7), custom_call_target="tpu_custom_call" | custom-call | flops 6710886400 | bytes 16777216 | tf_op jit(solution)/shard_map/pallas_call | solution.py:144
  177.9 0.7 collective-permute-start.1
  178.6 15.1 %shard_map.74 = bf16[128,4096]{1,0:T(8,128)(2,1)} custom-call(s32[5]{0:T(128)} %stack.83.plan_ref, bf16[512,1024]{1,0:T(8,128)(2,1)} %bitcast.45, bf16[128,128,512]{2,1,0:T(8,128)(2,1)} %bitcast.41, bf16[1024,4096]{1,0:T(8,128)(2,1)} %wo_hbm.7), custom_call_target="tpu_custom_call" | custom-call | flops 6710886400 | bytes 16777216 | tf_op jit(solution)/shard_map/pallas_call | solution.py:144
  193.7 2.7 %collective-permute-start = (bf16[128,4096]{1,0:T(8,128)(2,1)}, bf16[128,4096]{1,0:T(8,128)(2,1)}, u32[]{:S(2)}, u32[]{:S(2)}) collective-permute-start(bf16[128,4096]{1,0:T(8,128)(2,1)} %shard_map.74), channel_id=1, source_target_pairs={{0,3},{1,0},{2,1},{3,2},{4,7},{5,4},{6,5},{7,6},{8,11},{9,8},{10,9... | collective-permute-start | bytes 3145736 | tf_op jit(solution)/shard_map/ppermute | solution.py:207
  198.9 1.3 stack.77.plan_ref
  200.1 15.2 %shard_map.73 = bf16[128,4096]{1,0:T(8,128)(2,1)} custom-call(s32[5]{0:T(128)} %stack.77.plan_ref, bf16[512,1024]{1,0:T(8,128)(2,1)} %bitcast.46, bf16[128,128,512]{2,1,0:T(8,128)(2,1)} %bitcast.42, bf16[1024,4096]{1,0:T(8,128)(2,1)} %wo_hbm.7), custom_call_target="tpu_custom_call" | custom-call | flops 6710886400 | bytes 16777216 | tf_op jit(solution)/shard_map/pallas_call | solution.py:144
  215.4 3.5 %collective-permute-done = bf16[128,4096]{1,0:T(8,128)(2,1)} collective-permute-done((bf16[128,4096]{1,0:T(8,128)(2,1)}, bf16[128,4096]{1,0:T(8,128)(2,1)}, u32[]{:S(2)}, u32[]{:S(2)}) %collective-permute-start) | collective-permute-done | bytes 1048608 | tf_op jit(solution)/shard_map/ppermute | solution.py:207
  218.9 3.5 %add_convert_fusion = bf16[128,4096]{1,0:T(8,128)(2,1)} fusion(bf16[128,4096]{1,0:T(8,128)(2,1)S(1)} %collective-permute-done.2, bf16[128,4096]{1,0:T(8,128)(2,1)} %collective-permute-done.1, bf16[128,4096]{1,0:T(8,128)(2,1)} %collective-permute-done, bf16[128,4096]{1,0:T(8,128)(2,1)} %shard_map.73), kind=kLoop, calls=%fused_computation.7 | loop fusion | flops 4194304 | bytes 5242880 | tf_op jit(solution)/shard_map/convert_element_type | solution.py:210
  (22 shorter events, 0.9 us)
Async XLA Ops:
  6.5 55.2 %copy-start = (bf16[4096,256]{1,0:T(8,128)(2,1)S(1)}, bf16[4096,256]{1,0:T(8,128)(2,1)}, u32[]{:S(2)}) copy-start(bf16[4096,256]{1,0:T(8,128)(2,1)} %param.10) | copy-start | bytes 6291460
  6.5 4.3 %copy-start.2 = (s32[128]{0:T(128)S(1)}, s32[128]{0:T(128)}, u32[]{:S(2)}) copy-start(s32[128]{0:T(128)} %param.13) | copy-start | bytes 1540
  6.5 55.2 %all-gather.3.cloned.1.call-start = ((), (), s32[]{:S(2)}) async-start(), calls=%async_computation | async-start | bytes 5242880 | tf_op jit(solution)/shard_map/all_gather | solution.py:184
  10.8 133.6 %all-gather.5.cloned.1.call-start = ((), (), s32[]{:S(2)}) async-start(), calls=%async_computation.1 | async-start | bytes 17301504 | tf_op jit(solution)/shard_map/all_gather | solution.py:193
  65.8 1.6 copy-start.3
  159.5 55.9 %collective-permute-start.2 = (bf16[128,4096]{1,0:T(8,128)(2,1)}, bf16[128,4096]{1,0:T(8,128)(2,1)S(1)}, u32[]{:S(2)}, u32[]{:S(2)}) collective-permute-start(bf16[128,4096]{1,0:T(8,128)(2,1)} %shard_map.76), channel_id=1, source_target_pairs={{0,2},{1,3},{2,0},{3,1},{4,6},{5,7},{6,4},{7,5},{8,10},{9,11},{10,... | collective-permute-start | bytes 3145736 | tf_op jit(solution)/shard_map/ppermute | solution.py:207
  177.9 37.5 %collective-permute-start.1 = (bf16[128,4096]{1,0:T(8,128)(2,1)}, bf16[128,4096]{1,0:T(8,128)(2,1)}, u32[]{:S(2)}, u32[]{:S(2)}) collective-permute-start(bf16[128,4096]{1,0:T(8,128)(2,1)} %shard_map.75), channel_id=1, source_target_pairs={{0,1},{1,2},{2,3},{3,0},{4,5},{5,6},{6,7},{7,4},{8,9},{9,10},{10,1... | collective-permute-start | bytes 3145736 | tf_op jit(solution)/shard_map/ppermute | solution.py:207
  193.7 25.3 %collective-permute-start = (bf16[128,4096]{1,0:T(8,128)(2,1)}, bf16[128,4096]{1,0:T(8,128)(2,1)}, u32[]{:S(2)}, u32[]{:S(2)}) collective-permute-start(bf16[128,4096]{1,0:T(8,128)(2,1)} %shard_map.74), channel_id=1, source_target_pairs={{0,3},{1,0},{2,1},{3,2},{4,7},{5,4},{6,5},{7,6},{8,11},{9,8},{10,9... | collective-permute-start | bytes 3145736 | tf_op jit(solution)/shard_map/ppermute | solution.py:207
  200.1 22.3 %copy-start.1 = (bf16[4096,256]{1,0:T(8,128)(2,1)S(1)}, bf16[4096,256]{1,0:T(8,128)(2,1)}, u32[]{:S(2)}) copy-start(bf16[4096,256]{1,0:T(8,128)(2,1)} %param.10) | copy-start | bytes 6291460
Sparse Core Ops, SparseCore 0:
  10.9 50.8 all-gather.2
  71.8 72.5 all-gather.4
